TPU v7x, 256 devices: a whole 4x4x8 slice. The times are simulated.
256 devices in a mesh: ta: 16 (over x, z_hi), sa: 16 (over y, z_lo, core).
Axes of the slice: x: 4, y: 4, z: 8 (z_hi: 4, z_lo: 2; z = z_hi * 2 + z_lo), core: 2. Of those that a mesh axis runs over, the one named last changes fastest.
Arguments:
- temporal_links: float32 [18, 64, 32, 384], P(None, 'ta', 'sa'), may hold values from -1 to 1, as said below
- spatial_links: float32 [3, 18, 64, 32, 384], P(None, None, 'ta', 'sa'), may hold values from -1 to 1, as said below
- rotations: float32 [3, 3, 4, 64, 32, 384], P(None, None, None, 'ta', 'sa'), may hold values from -1 to 1, as said below
Outputs:
- transfer: float32 [2, 9, 9, 16, 32, 384], P(None, None, None, 'ta', 'sa')
- log_scale: float32 [16, 32, 384], P('ta', 'sa')
Inputs may be any that keep to these rules, and one draw needn't show every extreme that they name: `temporal_links`: every link's 3x3 complex matrix is special unitary. `spatial_links`: every link's 3x3 complex matrix is special unitary. `rotations`: the four entries along the third dimension form a unit quaternion.
All inputs are finite; a program needn't handle non-finite values.
Results may differ from a plain program's by a relative error of at most 0.0003.
Values sent between devices are 32-bit elements; how exact they have to be, the bound alone decides.
A program may use at most 128 MiB of HBM per device.

v0:
```python
import jax
import jax.numpy as jnp
from jax import lax
from jax.experimental import pallas as pl
from jax.experimental.pallas import tpu as pltpu
from jax.sharding import Mesh
from jax.sharding import PartitionSpec as P

SWEEPS = 3
LZ = 16
LANES = 128
MESH = pl.DeviceIdType.MESH
AXES = ("ta_0", "ta_1", "sa")
PLANES = ((0, 1), (1, 2), (0, 2))


def times(left, right):
    out_re, out_im = [], []
    for row in range(3):
        for col in range(3):
            re = im = None
            for mid in range(3):
                a_re, a_im = left[0][3 * row + mid], left[1][3 * row + mid]
                b_re, b_im = right[0][3 * mid + col], right[1][3 * mid + col]
                p_re = a_re * b_re - a_im * b_im
                p_im = a_re * b_im + a_im * b_re
                re = p_re if re is None else re + p_re
                im = p_im if im is None else im + p_im
            out_re.append(re)
            out_im.append(im)
    return out_re, out_im


def staple_term(total, later, now, link):
    total_re, total_im = list(total[0]), list(total[1])
    for col in range(3):
        mid_re, mid_im = [], []
        for k in range(3):
            re = im = None
            for m in range(3):
                a_re, a_im = now[0][3 * col + m], now[1][3 * col + m]
                b_re, b_im = link[0][3 * m + k], link[1][3 * m + k]
                p_re = a_re * b_re - a_im * b_im
                p_im = a_re * b_im + a_im * b_re
                re = p_re if re is None else re + p_re
                im = p_im if im is None else im + p_im
            mid_re.append(re)
            mid_im.append(im)
        for row in range(3):
            re, im = total_re[3 * row + col], total_im[3 * row + col]
            for k in range(3):
                a_re, a_im = later[0][3 * row + k], later[1][3 * row + k]
                p_re = a_re * mid_re[k] + a_im * mid_im[k]
                p_im = a_im * mid_re[k] - a_re * mid_im[k]
                re = p_re if re is None else re + p_re
                im = p_im if im is None else im + p_im
            total_re[3 * row + col], total_im[3 * row + col] = re, im
    return total_re, total_im


def dagger(matrix):
    order = (0, 3, 6, 1, 4, 7, 2, 5, 8)
    return [matrix[0][k] for k in order], [-matrix[1][k] for k in order]


def rotate_rows(matrix, upper, lower, quat):
    q0, q1, q2, q3 = quat
    re, im = list(matrix[0]), list(matrix[1])
    for col in range(3):
        u_re, u_im = matrix[0][3 * upper + col], matrix[1][3 * upper + col]
        l_re, l_im = matrix[0][3 * lower + col], matrix[1][3 * lower + col]
        re[3 * upper + col] = q0 * u_re - q3 * u_im + q2 * l_re - q1 * l_im
        im[3 * upper + col] = q0 * u_im + q3 * u_re + q2 * l_im + q1 * l_re
        re[3 * lower + col] = q0 * l_re + q3 * l_im - q2 * u_re - q1 * u_im
        im[3 * lower + col] = q0 * l_im - q3 * l_re - q2 * u_im + q1 * u_re
    return re, im


def reflected(product, upper, lower, turn):
    re, im = product
    uu, ul, lu, ll = 4 * upper, 3 * upper + lower, 3 * lower + upper, 4 * lower
    w0 = 0.5 * (re[uu] + re[ll])
    w1 = 0.5 * (im[ul] + im[lu])
    w2 = 0.5 * (re[ul] - re[lu])
    w3 = 0.5 * (im[uu] - im[ll])
    vec_sq = w1 * w1 + w2 * w2 + w3 * w3
    w0_sq = w0 * w0
    inv = 1.0 / jnp.maximum(w0_sq + vec_sq, 0.5)
    scale = -2.0 * w0 * inv
    r0, r1, r2, r3 = (w0_sq - vec_sq) * inv, scale * w1, scale * w2, scale * w3
    x0, x1, x2, x3 = turn
    return (
        x0 * r0 - (x1 * r1 + x2 * r2 + x3 * r3),
        x0 * r1 + r0 * x1 - (x2 * r3 - x3 * r2),
        x0 * r2 + r0 * x2 - (x3 * r1 - x1 * r3),
        x0 * r3 + r0 * x3 - (x1 * r2 - x2 * r1),
    )


def turn_lanes(value, steps):
    return pltpu.roll(value, (-steps) % LANES, 1)


def turn_rows(value, steps):
    return pltpu.roll(value, (-steps) % 8, 0)


class Shifts:
    def __init__(self):
        lane = lax.broadcasted_iota(jnp.int32, (8, LANES), 1)
        row = lax.broadcasted_iota(jnp.int32, (8, LANES), 0)
        self.depth = lane % LZ
        self.lane = lane
        self.slot = row % 4
        self.odd = ((lane // LZ + lane) % 2) == 1
        self.low_rows = row < 4
        self.even_lane = lane % 2 == 0

    def rows(self, value, offset):
        if offset > 0:
            turned = turn_lanes(value, LZ)
            after = jnp.where(self.slot == 2, turn_rows(turned, -2), turn_rows(turned, 1))
            return jnp.where(self.lane < LANES - LZ, turned, after)
        turned = turn_lanes(value, -LZ)
        before = jnp.where(self.slot == 0, turn_rows(turned, 2), turn_rows(turned, -1))
        return jnp.where(self.lane >= LZ, turned, before)

    def deep(self, value, offset):
        if offset > 0:
            return jnp.where(
                self.depth < LZ - offset, turn_lanes(value, offset), turn_lanes(value, offset - LZ)
            )
        return jnp.where(
            self.depth >= -offset, turn_lanes(value, offset), turn_lanes(value, LZ + offset)
        )

    def pair_swap(self, value):
        return jnp.where(self.even_lane, turn_lanes(value, 1), turn_lanes(value, -1))


def kernel(
    time_hbm, space_hbm, turn_hbm, out_ref,
    time_raw, space_raw, left_raw, halo_raw, turn_raw,
    field, bonds, shifted, pack_out, pack_in, loop_rows, loop_out, loop_in,
    oper, chain_a, chain_b, group, part, final,
    in_sem, edge_out, edge_in, halo_out, halo_in, loop_sent, loop_got, local_sem, back_sem, done_sem,
):
    ix, iz, ia = lax.axis_index("ta_0"), lax.axis_index("ta_1"), lax.axis_index("sa")
    nx, nz, na = 4, 4, lax.axis_size("sa")
    left, right = lax.rem(ia + na - 1, na), lax.rem(ia + 1, na)
    slab = ix * nz + iz
    earlier = lax.rem(slab + nx * nz - 1, nx * nz)
    later = lax.rem(slab + 1, nx * nz)
    earlier_x, earlier_z = earlier // nz, lax.rem(earlier, nz)
    later_x, later_z = later // nz, lax.rem(later, nz)

    local = []
    for t in range(4):
        for j in range(3):
            lanes, rows = pl.ds(LANES * j, LANES), pl.ds(8 * t + 2 * j, 2)
            local.append(pltpu.make_async_copy(
                time_hbm.at[:, t, :, lanes], time_raw.at[:, rows, :], in_sem.at[0]))
            local.append(pltpu.make_async_copy(
                space_hbm.at[:, :, t, :, lanes], space_raw.at[:, :, rows, :], in_sem.at[1]))
            local.append(pltpu.make_async_copy(
                turn_hbm.at[:, :, :, t, :, lanes], turn_raw.at[:, :, :, rows, :], in_sem.at[2]))
    for copy in local:
        copy.start()

    barrier = pltpu.get_barrier_semaphore()
    peers = []
    for step in range(1, nx * nz):
        peer = lax.rem(slab + step, nx * nz)
        peers.append((peer // nz, lax.rem(peer, nz), ia))
    peers += [(ix, iz, left), (ix, iz, right)]
    peers += [(earlier_x, earlier_z, right), (later_x, later_z, left)]
    for peer in peers:
        pl.semaphore_signal(barrier, inc=1, device_id=peer, device_id_type=MESH)
    pl.semaphore_wait(barrier, len(peers))

    def remote(src, dst, out_sem, got_sem, target):
        return pltpu.make_async_remote_copy(
            src_ref=src, dst_ref=dst, send_sem=out_sem, recv_sem=got_sem,
            device_id=target, device_id_type=MESH)

    def edge(group, src, dst, target):
        return remote(src, dst, edge_out.at[group], edge_in.at[group], target)

    def landed(ref, sem):
        pltpu.make_async_copy(ref, ref, sem).wait()

    edges = []
    for t in range(4):
        for j in range(3):
            lanes = pl.ds(LANES * j, LANES)
            low, high = pl.ds(8 * t + 2 * j, 1), pl.ds(8 * t + 2 * j + 1, 1)
            edges.append(edge(
                0, time_hbm.at[:, t, pl.ds(0, 1), lanes], halo_raw.at[:, low, :], (ix, iz, left)))
            edges.append(edge(
                1, time_hbm.at[:, t, pl.ds(1, 1), lanes], halo_raw.at[:, high, :], (ix, iz, right)))
            edges.append(edge(
                2, space_hbm.at[0, :, t, pl.ds(1, 1), lanes], left_raw.at[:, high, :],
                (ix, iz, right)))
    for j in range(3):
        lanes = pl.ds(LANES * j, LANES)
        edges.append(edge(
            3, space_hbm.at[:, :, 0, :, lanes], space_raw.at[:, :, pl.ds(32 + 2 * j, 2), :],
            (earlier_x, earlier_z, ia)))
        edges.append(edge(
            4, space_hbm.at[0, :, 0, pl.ds(1, 1), lanes],
            left_raw.at[:, pl.ds(32 + 2 * j + 1, 1), :], (earlier_x, earlier_z, right)))
    covers = (
        halo_raw.at[:, pl.ds(0, 12), :], halo_raw.at[:, pl.ds(0, 12), :],
        halo_raw.at[:, pl.ds(0, 12), :], space_raw.at[:, :, pl.ds(0, 6), :],
        halo_raw.at[:, pl.ds(0, 3), :])
    for copy in edges:
        copy.start()

    shifts = Shifts()
    odd = shifts.odd

    def own(parity, first, second):
        return jnp.where(odd, first, second) if parity else jnp.where(odd, second, first)

    landed(time_raw.at[:, pl.ds(0, 24), :], in_sem.at[0])
    landed(space_raw.at[:, :, pl.ds(0, 24), :], in_sem.at[1])
    landed(turn_raw.at[:, :, :, pl.ds(0, 24), :], in_sem.at[2])
    for block in range(2):
        for entry in range(18):
            first = time_raw[entry, pl.ds(16 * block, 8, stride=2), :]
            second = time_raw[entry, pl.ds(16 * block + 1, 8, stride=2), :]
            field[0, entry, pl.ds(8 * block, 8), :] = own(0, first, second)
            field[1, entry, pl.ds(8 * block, 8), :] = own(1, first, second)
    for group_idx, cover in enumerate(covers):
        landed(cover, edge_in.at[group_idx])

    @pl.loop(0, 3)
    def _(block):
        at = pl.multiple_of(16 * block, 16)
        to = pl.ds(pl.multiple_of(8 * block, 8), 8)

        def raw(ref, lead, column):
            return [ref[(*lead, k, pl.ds(at + column, 8, stride=2), slice(None))] for k in range(18)]

        def put(parity, place, matrix):
            for k in range(9):
                bonds[parity, place, k, to, :] = matrix[0][k]
                bonds[parity, place, 9 + k, to, :] = matrix[1][k]

        def split(values):
            return values[:9], values[9:]

        inner, outer, beyond = (
            raw(space_raw, (0,), 0), raw(space_raw, (0,), 1), raw(left_raw, (), 1))
        inner_dag, beyond_dag = dagger(split(inner)), dagger(split(beyond))
        inner_dag, beyond_dag = inner_dag[0] + inner_dag[1], beyond_dag[0] + beyond_dag[1]
        for parity in (0, 1):
            put(parity, 0, split([own(parity, a, b) for a, b in zip(inner, inner_dag)]))
            put(parity, 5, split([own(parity, a, b) for a, b in zip(beyond_dag, outer)]))
        for direction, shift in ((1, shifts.rows), (2, shifts.deep)):
            first, second = raw(space_raw, (direction,), 0), raw(space_raw, (direction,), 1)
            for parity in (0, 1):
                here = [own(parity, a, b) for a, b in zip(first, second)]
                put(parity, 2 * direction - 1, split(here))
                back = [shift(value, -1) for value in here]
                put(1 - parity, 2 * direction, dagger(split(back)))

    def half_sweep(sweep, parity):
        number = 2 * sweep + parity

        @pl.loop(0, 2)
        def _(block):
            rows = pl.ds(pl.multiple_of(8 * block, 8), 8)
            rows_later = pl.ds(8 * block + 4, 8)

            def load(ref, lead, where):
                values = [ref[(*lead, k, where, slice(None))] for k in range(18)]
                return values[:9], values[9:]

            for entry in range(18):
                value = field[1 - parity, entry, rows, :]
                shifted[0, entry] = shifts.rows(value, 1)
                shifted[1, entry] = shifts.rows(value, -1)
                shifted[2, entry] = shifts.deep(value, 1)
                shifted[3, entry] = shifts.deep(value, -1)
            total = ([None] * 9, [None] * 9)
            total = staple_term(
                total, load(bonds, (parity, 0), rows_later), load(bonds, (parity, 0), rows),
                load(field, (1 - parity,), rows))
            for place in range(1, 5):
                total = staple_term(
                    total, load(bonds, (parity, place), rows_later),
                    load(bonds, (parity, place), rows),
                    load(shifted, (place - 1,), slice(None)))
            for k in range(9):
                shifted[4, k] = total[0][k]
                shifted[4, 9 + k] = total[1][k]

            @pl.when(number == 0)
            def _():
                base = pl.multiple_of(16 * block, 16)
                for entry in range(18):
                    from_right = halo_raw[entry, pl.ds(base, 8, stride=2), :]
                    from_left = halo_raw[entry, pl.ds(base + 1, 8, stride=2), :]
                    shifted[5, entry] = own(parity, from_left, from_right)

            @pl.when(number > 0)
            def _():
                for side in range(2):
                    remote(
                        pack_out.at[number - 1, block, side], pack_in.at[number - 1, block, side],
                        halo_out.at[number - 1, block, side], halo_in.at[number - 1, block, side],
                        (ix, iz, left)).wait_recv()
                for k in range(9):
                    from_left = pack_in[number - 1, block, 1, k]
                    from_right = pack_in[number - 1, block, 0, k]
                    shifted[5, k] = own(parity, from_left, from_right)
                    shifted[5, 9 + k] = shifts.pair_swap(own(parity, from_right, from_left))

            total = load(shifted, (4,), slice(None))
            total = staple_term(
                total, load(bonds, (parity, 5), rows_later), load(bonds, (parity, 5), rows),
                load(shifted, (5,), slice(None)))
            links = load(field, (parity,), rows)
            product = times(links, total)
            for plane, (upper, lower) in enumerate(PLANES):
                base = pl.multiple_of(16 * block, 16)
                turn = [
                    own(parity, turn_raw[sweep, plane, k, pl.ds(base, 8, stride=2), :],
                        turn_raw[sweep, plane, k, pl.ds(base + 1, 8, stride=2), :])
                    for k in range(4)]
                quat = reflected(product, upper, lower, turn)
                links = rotate_rows(links, upper, lower, quat)
                if plane < 2:
                    product = rotate_rows(product, upper, lower, quat)
            for k in range(9):
                field[parity, k, rows, :] = links[0][k]
                field[parity, 9 + k, rows, :] = links[1][k]

            @pl.when(number < 2 * SWEEPS - 1)
            def _():
                for k in range(9):
                    real, partner = links[0][k], shifts.pair_swap(links[1][k])
                    pack_out[number, block, 0, k] = own(parity, real, partner)
                    pack_out[number, block, 1, k] = own(parity, partner, real)
                for side, target in ((0, left), (1, right)):
                    remote(
                        pack_out.at[number, block, side], pack_in.at[number, block, side],
                        halo_out.at[number, block, side], halo_in.at[number, block, side],
                        (ix, iz, target)).start()

    def send_loops(sweep):
        low = shifts.low_rows
        stage = []
        for parity in (0, 1):
            even, odd_t = [], []
            for entry in range(18):
                a = field[parity, entry, pl.ds(0, 8), :]
                b = field[parity, entry, pl.ds(4, 8), :]
                c = field[parity, entry, pl.ds(8, 8), :]
                even.append(jnp.where(low, a, b))
                odd_t.append(jnp.where(low, b, c))
            stage.append(times((even[:9], even[9:]), (odd_t[:9], odd_t[9:])))
        head, tail = [], []
        for part_idx in (0, 1):
            for k in range(9):
                a, b = stage[0][part_idx][k], stage[1][part_idx][k]
                head.append(jnp.where(low, a, turn_rows(b, 4)))
                tail.append(jnp.where(low, turn_rows(a, 4), b))
        loops = times((head[:9], head[9:]), (tail[:9], tail[9:]))
        for entry, value in enumerate(loops[0] + loops[1]):
            loop_rows[entry] = own(0, value, turn_rows(value, 4))
            for j in range(4):
                loop_out[sweep, entry, pl.ds(2 * j, 2), :] = (
                    loop_rows[entry, pl.ds(j, 2, stride=4), :])
        for step in range(nx * nz):
            if step == 0:
                @pl.when(ix > 0)
                def _():
                    pltpu.make_async_copy(
                        loop_out.at[sweep, :, pl.ds(2 * (ix - 1), 2), :],
                        loop_in.at[sweep, iz, :, pl.ds(2 * ix, 2), :], local_sem.at[sweep]).start()
            else:
                peer = lax.rem(slab + step, nx * nz)
                peer_x, peer_z = peer // nz, lax.rem(peer, nz)

                @pl.when(peer_x > 0)
                def _():
                    remote(
                        loop_out.at[sweep, :, pl.ds(2 * (peer_x - 1), 2), :],
                        loop_in.at[sweep, iz, :, pl.ds(2 * ix, 2), :],
                        loop_sent.at[sweep], loop_got.at[sweep], (peer_x, peer_z, ia)).start()

    @pl.loop(0, SWEEPS)
    def _(sweep):
        half_sweep(sweep, 0)
        half_sweep(sweep, 1)
        send_loops(sweep)

    def normalized(load, store, log):
        square = None
        for k in range(162):
            value = load(k)
            square = value * value if square is None else square + value * value
        rms = jnp.sqrt(square / 162.0 + 1e-06)
        inv = 1.0 / rms
        for k in range(162):
            store(k, load(k) * inv)
        return log + jnp.log(rms)

    def combine(left_ref, right_ref, dst_ref, keep):
        @pl.loop(0, 9)
        def _(row):
            for half in range(3):
                columns = range(3 * half, 3 * half + 3)
                re, im = [None] * 3, [None] * 3
                for mid in range(9):
                    a_re, a_im = left_ref[9 * row + mid], left_ref[81 + 9 * row + mid]
                    for place, col in enumerate(columns):
                        b_re, b_im = right_ref[9 * mid + col], right_ref[81 + 9 * mid + col]
                        p_re = a_re * b_re - a_im * b_im
                        p_im = a_re * b_im + a_im * b_re
                        re[place] = p_re if re[place] is None else re[place] + p_re
                        im[place] = p_im if im[place] is None else im[place] + p_im
                for place, col in enumerate(columns):
                    dst_ref[9 * row + col] = re[place]
                    dst_ref[81 + 9 * row + col] = im[place]
        log = normalized(
            lambda k: dst_ref[k], lambda k, value: dst_ref.__setitem__(k, keep(k, value)),
            left_ref[162] + right_ref[162])
        dst_ref[162] = keep(162, log)

    @pl.when(ix > 0)
    def _():
        for sweep in range(SWEEPS):
            pltpu.make_async_copy(
                loop_out.at[sweep, :, pl.ds(2 * (ix - 1), 2), :],
                loop_in.at[sweep, iz, :, pl.ds(2 * ix, 2), :], local_sem.at[sweep]).wait()
            landed(space_raw.at[0, :, pl.ds(0, 30), :], loop_got.at[sweep])

        @pl.loop(0, nz)
        def _(slot):
            for sweep in range(SWEEPS):
                loops = [loop_in[sweep, slot, k] for k in range(18)]
                partner = [shifts.deep(value, 4) for value in loops]
                for a in range(3):
                    for c in range(3):
                        for e in range(3):
                            for d in range(3):
                                l_re, l_im = loops[3 * a + e], loops[9 + 3 * a + e]
                                r_re, r_im = partner[3 * c + d], partner[9 + 3 * c + d]
                                re = l_re * r_re + l_im * r_im
                                im = l_im * r_re - l_re * r_im
                                at = 9 * (3 * a + c) + 3 * e + d
                                if sweep:
                                    re = oper[slot, at] + re
                                    im = oper[slot, 81 + at] + im
                                oper[slot, at] = re
                                oper[slot, 81 + at] = im
            third = 1.0 / SWEEPS
            log = normalized(
                lambda k: oper[slot, k] * third,
                lambda k, value: oper.at[slot].__setitem__(k, value), jnp.zeros((8, LANES)))
            oper[slot, 162] = log

        @pl.loop(0, 163)
        def _(k):
            part[0, k] = oper[0, k]

        @pl.loop(1, nz)
        def _(slot):
            combine(part.at[slot - 1], oper.at[slot], part.at[slot], lambda k, value: value)

        row = lax.broadcasted_iota(jnp.int32, (8, LANES), 0)

        def moved(value, k, rows):
            unit = 1.0 if k < 81 and k % 10 == 0 else 0.0
            return jnp.where(row < rows, unit, turn_rows(value, -rows))

        for k in range(163):
            chain_a[k] = moved(part[nz - 1, k], k, 2)
            chain_b[k] = moved(chain_a[k], k, 2)
        combine(chain_b, chain_a, group, lambda k, value: jnp.where(row < 2, chain_a[k], value))
        for k in range(163):
            chain_b[k] = moved(group[k], k, 4)
        combine(chain_b, group, chain_a, lambda k, value: jnp.where(row < 4, group[k], value))
        combine(chain_a, part.at[iz], final, lambda k, value: value)

        for target in range(nx):
            src = final.at[:, pl.ds(2 * target, 2), :]
            dst = out_ref.at[:, ix - 1]

            @pl.when(ix == target)
            def _():
                pltpu.make_async_copy(src, dst, done_sem.at[0]).start()

            @pl.when(ix != target)
            def _():
                pltpu.make_async_remote_copy(
                    src_ref=src, dst_ref=dst, send_sem=done_sem.at[1], recv_sem=back_sem.at[ix],
                    device_id=(target, iz, ia), device_id_type=MESH).start()
        pltpu.make_async_copy(
            final.at[:, pl.ds(0, 2), :], out_ref.at[:, 0], done_sem.at[0]).wait()

    for source in range(1, nx):
        @pl.when(ix != source)
        def _():
            remote(
                final.at[:, pl.ds(0, 2), :], out_ref.at[:, 0], done_sem.at[1], back_sem.at[source],
                (ix, iz, left)).wait_recv()

    for group_idx, cover in enumerate(covers):
        landed(cover, edge_out.at[group_idx])
    for number in range(2 * SWEEPS - 1):
        for block in range(2):
            for side in range(2):
                landed(pack_out.at[number, block, side], halo_out.at[number, block, side])

    @pl.when(ix == 0)
    def _():
        for sweep in range(SWEEPS):
            landed(space_raw.at[0, :, pl.ds(0, 24), :], loop_sent.at[sweep])

    @pl.when(ix > 0)
    def _():
        for sweep in range(SWEEPS):
            landed(space_raw.at[0, :, pl.ds(0, 22), :], loop_sent.at[sweep])
        landed(final.at[:, pl.ds(0, 6), :], done_sem.at[1])


def per_device(temporal_links, spatial_links, rotations):
    f32, dma = jnp.float32, pltpu.SemaphoreType.DMA
    halves = 2 * SWEEPS - 1
    out = pl.pallas_call(
        kernel,
        name="slab_chain",
        out_shape=jax.ShapeDtypeStruct((163, 3, 2, LANES), f32),
        in_specs=[pl.BlockSpec(memory_space=pl.ANY)] * 3,
        out_specs=pl.BlockSpec(memory_space=pltpu.VMEM),
        scratch_shapes=[
            pltpu.VMEM((18, 32, LANES), f32),
            pltpu.VMEM((3, 18, 48, LANES), f32),
            pltpu.VMEM((18, 48, LANES), f32),
            pltpu.VMEM((18, 32, LANES), f32),
            pltpu.VMEM((3, 3, 4, 32, LANES), f32),
            pltpu.VMEM((2, 18, 16, LANES), f32),
            pltpu.VMEM((2, 6, 18, 24, LANES), f32),
            pltpu.VMEM((6, 18, 8, LANES), f32),
            pltpu.VMEM((halves, 2, 2, 9, 8, LANES), f32),
            pltpu.VMEM((halves, 2, 2, 9, 8, LANES), f32),
            pltpu.VMEM((18, 8, LANES), f32),
            pltpu.VMEM((SWEEPS, 18, 8, LANES), f32),
            pltpu.VMEM((SWEEPS, 4, 18, 8, LANES), f32),
            pltpu.VMEM((4, 163, 8, LANES), f32),
            pltpu.VMEM((163, 8, LANES), f32),
            pltpu.VMEM((163, 8, LANES), f32),
            pltpu.VMEM((163, 8, LANES), f32),
            pltpu.VMEM((4, 163, 8, LANES), f32),
            pltpu.VMEM((163, 8, LANES), f32),
            dma((3,)), dma((5,)), dma((5,)), dma((halves, 2, 2)), dma((halves, 2, 2)),
            dma((SWEEPS,)), dma((SWEEPS,)), dma((SWEEPS,)), dma((4,)), dma((2,)),
        ],
        compiler_params=pltpu.CompilerParams(collective_id=0, has_side_effects=True),
    )(temporal_links, spatial_links, rotations)
    transfer = out[:162].reshape(2, 9, 9, 3, 2, LANES).transpose(0, 1, 2, 4, 3, 5)
    log_scale = out[162].transpose(1, 0, 2).reshape(1, 2, 3 * LANES)
    return transfer.reshape(2, 9, 9, 1, 2, 3 * LANES), log_scale


def solution(mesh):
    split = Mesh(mesh.devices.reshape(4, 4, mesh.shape["sa"]), AXES)
    slabs = ("ta_0", "ta_1")
    return jax.shard_map(
        per_device,
        mesh=split,
        in_specs=(
            P(None, slabs, "sa", None),
            P(None, None, slabs, "sa", None),
            P(None, None, None, slabs, "sa", None),
        ),
        out_specs=(P(None, None, None, slabs, "sa", None), P(slabs, "sa", None)),
        check_vma=False,
    )
```

profile of v0, /device:TPU:6, one launch (start us, length us, event | category | flops | bytes accessed | tf_op | source)
XLA Modules:
  0.0 78.5 jit_solution(16203170818108201899)
XLA Ops:
  0.6 74.2 %slab_chain.1 = f32[163,3,2,128]{3,2,1,0:T(2,128)} custom-call(f32[18,4,2,384]{3,2,1,0:T(2,128)} %time_hbm.1, f32[3,18,4,2,384]{4,3,2,1,0:T(2,128)} %space_hbm.1, f32[3,3,4,4,2,384]{5,4,3,2,1,0:T(2,128)} %turn_hbm.1), custom_call_target="tpu_custom_call" | custom-call | tf_op jit(solution)/shard_map/slab_chain/pallas_call | solution.py:534
  74.9 1.2 %slice_bitcast_fusion = f32[1,2,384]{2,1,0:T(2,128)} fusion(f32[163,3,2,128]{3,2,1,0:T(2,128)} %slab_chain.1), kind=kLoop, calls=%fused_computation.1 | loop fusion | bytes 6144 | tf_op jit(solution)/shard_map/reshape | solution.py:566
  76.1 0.0 slice-start
  76.1 1.0 %slice-done = f32[162,3,2,128]{3,2,1,0:T(2,128)S(1)} async-done(((f32[163,3,2,128]{3,2,1,0:T(2,128)}), f32[162,3,2,128]{3,2,1,0:T(2,128)S(1)}, s32[]{:S(2)}) %slice-start) | async-done | bytes 497688 | tf_op jit(solution)/shard_map/slice | solution.py:565
  77.1 0.2 copy.9
  77.3 1.2 %reshape.14 = f32[2,9,9,1,2,384]{5,4,2,1,0,3:T(2,128)} reshape(f32[2,9,9,2,3,128]{5,4,3,2,1,0:T(4,128)S(1)} %bitcast.11) | data formatting | bytes 995328 | tf_op jit(solution)/shard_map/reshape | solution.py:567
Async XLA Ops:
  76.1 1.0 %slice-start = ((f32[163,3,2,128]{3,2,1,0:T(2,128)}), f32[162,3,2,128]{3,2,1,0:T(2,128)S(1)}, s32[]{:S(2)}) async-start(f32[163,3,2,128]{3,2,1,0:T(2,128)} %slab_chain.1), calls=%async_computation | async-start | bytes 995328 | tf_op jit(solution)/shard_map/slice | solution.py:565
where the time goes:
time: 79.9 us; the launch traced here: 78.5 us
  Pallas kernels  74.2 us (93%)
  local copies, waits for them, and re-layouts  3.66 us (5%)
    pallas_call x1, Pallas kernels, per_device(): pl.pallas_call(kernel, name='slab_chain', out_shape=jax.ShapeDtypeStruct(...  74.2 us

commit v1 on v0

v1 whole, which is shorter than its diff:
```python
import jax
import jax.numpy as jnp
from jax import lax
from jax.experimental import pallas as pl
from jax.experimental.pallas import tpu as pltpu
from jax.sharding import Mesh
from jax.sharding import PartitionSpec as P

SWEEPS = 3
LZ = 16
LANES = 128
MESH = pl.DeviceIdType.MESH
AXES = ("ta_0", "ta_1", "sa")
PLANES = ((0, 1), (1, 2), (0, 2))


def times(left, right):
    out_re, out_im = [], []
    for row in range(3):
        for col in range(3):
            re = im = None
            for mid in range(3):
                a_re, a_im = left[0][3 * row + mid], left[1][3 * row + mid]
                b_re, b_im = right[0][3 * mid + col], right[1][3 * mid + col]
                p_re = a_re * b_re - a_im * b_im
                p_im = a_re * b_im + a_im * b_re
                re = p_re if re is None else re + p_re
                im = p_im if im is None else im + p_im
            out_re.append(re)
            out_im.append(im)
    return out_re, out_im


def staple_term(total, later, now, link):
    total_re, total_im = list(total[0]), list(total[1])
    for col in range(3):
        mid_re, mid_im = [], []
        for k in range(3):
            re = im = None
            for m in range(3):
                a_re, a_im = now[0][3 * col + m], now[1][3 * col + m]
                b_re, b_im = link[0][3 * m + k], link[1][3 * m + k]
                p_re = a_re * b_re - a_im * b_im
                p_im = a_re * b_im + a_im * b_re
                re = p_re if re is None else re + p_re
                im = p_im if im is None else im + p_im
            mid_re.append(re)
            mid_im.append(im)
        for row in range(3):
            re, im = total_re[3 * row + col], total_im[3 * row + col]
            for k in range(3):
                a_re, a_im = later[0][3 * row + k], later[1][3 * row + k]
                p_re = a_re * mid_re[k] + a_im * mid_im[k]
                p_im = a_im * mid_re[k] - a_re * mid_im[k]
                re = p_re if re is None else re + p_re
                im = p_im if im is None else im + p_im
            total_re[3 * row + col], total_im[3 * row + col] = re, im
    return total_re, total_im


def dagger(matrix):
    order = (0, 3, 6, 1, 4, 7, 2, 5, 8)
    return [matrix[0][k] for k in order], [-matrix[1][k] for k in order]


def rotate_rows(matrix, upper, lower, quat):
    q0, q1, q2, q3 = quat
    re, im = list(matrix[0]), list(matrix[1])
    for col in range(3):
        u_re, u_im = matrix[0][3 * upper + col], matrix[1][3 * upper + col]
        l_re, l_im = matrix[0][3 * lower + col], matrix[1][3 * lower + col]
        re[3 * upper + col] = q0 * u_re - q3 * u_im + q2 * l_re - q1 * l_im
        im[3 * upper + col] = q0 * u_im + q3 * u_re + q2 * l_im + q1 * l_re
        re[3 * lower + col] = q0 * l_re + q3 * l_im - q2 * u_re - q1 * u_im
        im[3 * lower + col] = q0 * l_im - q3 * l_re - q2 * u_im + q1 * u_re
    return re, im


def reflected(product, upper, lower, turn):
    re, im = product
    uu, ul, lu, ll = 4 * upper, 3 * upper + lower, 3 * lower + upper, 4 * lower
    w0 = 0.5 * (re[uu] + re[ll])
    w1 = 0.5 * (im[ul] + im[lu])
    w2 = 0.5 * (re[ul] - re[lu])
    w3 = 0.5 * (im[uu] - im[ll])
    vec_sq = w1 * w1 + w2 * w2 + w3 * w3
    w0_sq = w0 * w0
    inv = 1.0 / jnp.maximum(w0_sq + vec_sq, 0.5)
    scale = -2.0 * w0 * inv
    r0, r1, r2, r3 = (w0_sq - vec_sq) * inv, scale * w1, scale * w2, scale * w3
    x0, x1, x2, x3 = turn
    return (
        x0 * r0 - (x1 * r1 + x2 * r2 + x3 * r3),
        x0 * r1 + r0 * x1 - (x2 * r3 - x3 * r2),
        x0 * r2 + r0 * x2 - (x3 * r1 - x1 * r3),
        x0 * r3 + r0 * x3 - (x1 * r2 - x2 * r1),
    )


def closed(six):
    re, im = list(six[0]), list(six[1])
    for col in range(3):
        a, b = (col + 1) % 3, (col + 2) % 3
        real = (re[a] * re[3 + b] - im[a] * im[3 + b]) - (re[b] * re[3 + a] - im[b] * im[3 + a])
        imag = (re[a] * im[3 + b] + im[a] * re[3 + b]) - (re[b] * im[3 + a] + im[b] * re[3 + a])
        re.append(real)
        im.append(-imag)
    return re, im


def turn_lanes(value, steps):
    return pltpu.roll(value, (-steps) % LANES, 1)


def turn_rows(value, steps):
    return pltpu.roll(value, (-steps) % 8, 0)


class Shifts:
    def __init__(self):
        lane = lax.broadcasted_iota(jnp.int32, (8, LANES), 1)
        row = lax.broadcasted_iota(jnp.int32, (8, LANES), 0)
        self.depth = lane % LZ
        self.lane = lane
        self.slot = row % 4
        self.odd = ((lane // LZ + lane) % 2) == 1
        self.low_rows = row < 4
        self.even_lane = lane % 2 == 0

    def rows(self, value, offset):
        if offset > 0:
            turned = turn_lanes(value, LZ)
            after = jnp.where(self.slot == 2, turn_rows(turned, -2), turn_rows(turned, 1))
            return jnp.where(self.lane < LANES - LZ, turned, after)
        turned = turn_lanes(value, -LZ)
        before = jnp.where(self.slot == 0, turn_rows(turned, 2), turn_rows(turned, -1))
        return jnp.where(self.lane >= LZ, turned, before)

    def deep(self, value, offset):
        if offset > 0:
            return jnp.where(
                self.depth < LZ - offset, turn_lanes(value, offset), turn_lanes(value, offset - LZ)
            )
        return jnp.where(
            self.depth >= -offset, turn_lanes(value, offset), turn_lanes(value, LZ + offset)
        )

    def pair_swap(self, value):
        return jnp.where(self.even_lane, turn_lanes(value, 1), turn_lanes(value, -1))


def kernel(
    time_hbm, space_hbm, turn_hbm, out_hbm, log_hbm,
    time_raw, space_raw, turn_raw, left_out, left_in, left_next,
    field, bonds, shifted, pack_out, pack_in, loop_rows, loop_out, loop_in,
    oper, chain_a, chain_b, group, part, final,
    in_sem, edge_out, edge_in, halo_out, halo_in, loop_sent, loop_got, local_sem, back_sem, done_sem,
):
    ix, iz, ia = lax.axis_index("ta_0"), lax.axis_index("ta_1"), lax.axis_index("sa")
    nx, nz, na = 4, 4, lax.axis_size("sa")
    left, right = lax.rem(ia + na - 1, na), lax.rem(ia + 1, na)
    slab = ix * nz + iz
    earlier = lax.rem(slab + nx * nz - 1, nx * nz)
    later = lax.rem(slab + 1, nx * nz)
    earlier_x, earlier_z = earlier // nz, lax.rem(earlier, nz)
    later_x, later_z = later // nz, lax.rem(later, nz)
    halves = 2 * SWEEPS

    for t in range(4):
        for j in range(3):
            lanes, rows = pl.ds(LANES * j, LANES), pl.ds(8 * t + 2 * j, 2)
            pltpu.make_async_copy(
                time_hbm.at[:, t, :, lanes], time_raw.at[:, rows, :], in_sem.at[0]).start()
            pltpu.make_async_copy(
                space_hbm.at[:, :, t, :, lanes], space_raw.at[:, :, rows, :], in_sem.at[1]).start()
    for t in range(4):
        for j in range(3):
            lanes, rows = pl.ds(LANES * j, LANES), pl.ds(8 * t + 2 * j, 2)
            pltpu.make_async_copy(
                turn_hbm.at[:, :, :, t, :, lanes], turn_raw.at[:, :, :, rows, :], in_sem.at[2]
            ).start()

    barrier = pltpu.get_barrier_semaphore()
    peers = []
    for step in range(1, nx * nz):
        peer = lax.rem(slab + step, nx * nz)
        peers.append((peer // nz, lax.rem(peer, nz), ia))
    peers += [(ix, iz, left), (ix, iz, right)]
    peers += [(earlier_x, earlier_z, right), (later_x, later_z, left)]
    for peer in peers:
        pl.semaphore_signal(barrier, inc=1, device_id=peer, device_id_type=MESH)

    def remote(src, dst, out_sem, got_sem, target):
        return pltpu.make_async_remote_copy(
            src_ref=src, dst_ref=dst, send_sem=out_sem, recv_sem=got_sem,
            device_id=target, device_id_type=MESH)

    def landed(ref, sem):
        pltpu.make_async_copy(ref, ref, sem).wait()

    shifts = Shifts()
    odd = shifts.odd

    def own(parity, first, second):
        return jnp.where(odd, first, second) if parity else jnp.where(odd, second, first)

    def split(values):
        return values[:9], values[9:]

    def pack(number, block, parity, links):
        for k in range(9):
            real, partner = links[0][k], shifts.pair_swap(links[1][k])
            pack_out[number, block, 0, k] = own(parity, real, partner)
            pack_out[number, block, 1, k] = own(parity, partner, real)

    def halo(number, block, side, target):
        return remote(
            pack_out.at[number, block, side], pack_in.at[number, block, side],
            halo_out.at[number, block, side], halo_in.at[number, block, side], (ix, iz, target))

    landed(time_raw.at[:, pl.ds(0, 24), :], in_sem.at[0])
    for block in range(2):
        packed = []
        for entry in range(18):
            first = time_raw[entry, pl.ds(16 * block, 8, stride=2), :]
            second = time_raw[entry, pl.ds(16 * block + 1, 8, stride=2), :]
            field[0, entry, pl.ds(8 * block, 8), :] = own(0, first, second)
            value = own(1, first, second)
            field[1, entry, pl.ds(8 * block, 8), :] = value
            packed.append(value)
        pack(0, block, 1, split(packed))
    landed(space_raw.at[:, :, pl.ds(0, 24), :], in_sem.at[1])
    two_rows = [*range(6), *range(9, 15)]
    for block in range(2):
        for place, entry in enumerate(two_rows):
            left_out[place, pl.ds(8 * block, 8), :] = (
                space_raw[0, entry, pl.ds(16 * block + 1, 8, stride=2), :])

    def raw(direction, at, column):
        return [space_raw[direction, k, pl.ds(at + column, 8, stride=2), :] for k in range(18)]

    def inner_bonds(block):
        at, to = 16 * block, pl.ds(8 * block, 8)
        if not isinstance(block, int):
            at, to = pl.multiple_of(at, 16), pl.ds(pl.multiple_of(8 * block, 8), 8)

        def put(parity, place, matrix):
            for k in range(9):
                bonds[parity, place, k, to, :] = matrix[0][k]
                bonds[parity, place, 9 + k, to, :] = matrix[1][k]

        inner = raw(0, at, 0)
        inner_dag = dagger(split(inner))
        inner_dag = inner_dag[0] + inner_dag[1]
        for parity in (0, 1):
            put(parity, 0, split([own(parity, a, b) for a, b in zip(inner, inner_dag)]))
        for direction, shift in ((1, shifts.rows), (2, shifts.deep)):
            first, second = raw(direction, at, 0), raw(direction, at, 1)
            for parity in (0, 1):
                here = [own(parity, a, b) for a, b in zip(first, second)]
                put(parity, 2 * direction - 1, split(here))
                back = [shift(value, -1) for value in here]
                put(1 - parity, 2 * direction, dagger(split(back)))

    def outer_bonds(block):
        to = pl.ds(8 * block, 8)
        outer = raw(0, 16 * block, 1)
        if block < 2:
            six = [left_in[k, to, :] for k in range(12)]
        else:
            six = [left_next[k, pl.ds(1, 8, stride=2), :] for k in range(12)]
        beyond = dagger(closed((six[:6], six[6:])))
        beyond = beyond[0] + beyond[1]
        for parity in (0, 1):
            for k in range(18):
                bonds[parity, 5, k, to, :] = own(parity, beyond[k], outer[k])

    @pl.loop(0, 2)
    def _(block):
        inner_bonds(block)

    pl.semaphore_wait(barrier, len(peers))
    for block in range(2):
        for side, target in ((0, left), (1, right)):
            halo(0, block, side, target).start()
    edges = [remote(left_out, left_in, edge_out.at[0], edge_in.at[0], (ix, iz, right))]
    for half in range(2):
        rows = pl.ds(0, 6)
        edges.append(remote(
            space_raw.at[:, pl.ds(9 * half, 6), rows, :],
            space_raw.at[:, pl.ds(9 * half, 6), pl.ds(32, 6), :],
            edge_out.at[1 + half], edge_in.at[1 + half], (earlier_x, earlier_z, ia)))
        edges.append(remote(
            space_raw.at[0, pl.ds(9 * half, 6), rows, :],
            left_next.at[pl.ds(6 * half, 6), rows, :],
            edge_out.at[3 + half], edge_in.at[3 + half], (earlier_x, earlier_z, right)))
    for copy in edges:
        copy.start()
    landed(turn_raw.at[:, :, :, pl.ds(0, 24), :], in_sem.at[2])
    edges[0].wait_recv()
    for block in range(2):
        outer_bonds(block)

    def half_sweep(sweep, parity):
        number = 2 * sweep + parity

        @pl.loop(0, 2)
        def _(block):
            rows = pl.ds(pl.multiple_of(8 * block, 8), 8)
            rows_later = pl.ds(8 * block + 4, 8)

            if parity == 0:
                @pl.when(jnp.logical_and(sweep == 0, block == 1))
                def _():
                    for copy in edges[1:]:
                        copy.wait_recv()
                    for direction in range(3):
                        six = [space_raw[direction, k, pl.ds(32, 8), :] for k in two_rows]
                        re, im = closed((six[:6], six[6:]))
                        for k in range(6, 9):
                            space_raw[direction, k, pl.ds(32, 8), :] = re[k]
                            space_raw[direction, 9 + k, pl.ds(32, 8), :] = im[k]
                    inner_bonds(2)
                    outer_bonds(2)

            def load(ref, lead, where):
                return split([ref[(*lead, k, where, slice(None))] for k in range(18)])

            for entry in range(18):
                value = field[1 - parity, entry, rows, :]
                shifted[0, entry] = shifts.rows(value, 1)
                shifted[1, entry] = shifts.rows(value, -1)
                shifted[2, entry] = shifts.deep(value, 1)
                shifted[3, entry] = shifts.deep(value, -1)
            total = ([None] * 9, [None] * 9)
            total = staple_term(
                total, load(bonds, (parity, 0), rows_later), load(bonds, (parity, 0), rows),
                load(field, (1 - parity,), rows))
            for place in range(1, 5):
                total = staple_term(
                    total, load(bonds, (parity, place), rows_later),
                    load(bonds, (parity, place), rows),
                    load(shifted, (place - 1,), slice(None)))

            for side in range(2):
                halo(number, block, side, left).wait_recv()
            beyond_re, beyond_im = [], []
            for k in range(9):
                from_left = pack_in[number, block, 1, k]
                from_right = pack_in[number, block, 0, k]
                beyond_re.append(own(parity, from_left, from_right))
                beyond_im.append(shifts.pair_swap(own(parity, from_right, from_left)))
            total = staple_term(
                total, load(bonds, (parity, 5), rows_later), load(bonds, (parity, 5), rows),
                (beyond_re, beyond_im))
            links = load(field, (parity,), rows)
            product = times(links, total)
            for plane, (upper, lower) in enumerate(PLANES):
                base = pl.multiple_of(16 * block, 16)
                turn = [
                    own(parity, turn_raw[sweep, plane, k, pl.ds(base, 8, stride=2), :],
                        turn_raw[sweep, plane, k, pl.ds(base + 1, 8, stride=2), :])
                    for k in range(4)]
                quat = reflected(product, upper, lower, turn)
                links = rotate_rows(links, upper, lower, quat)
                if plane < 2:
                    product = rotate_rows(product, upper, lower, quat)
            for k in range(9):
                field[parity, k, rows, :] = links[0][k]
                field[parity, 9 + k, rows, :] = links[1][k]

            @pl.when(number < halves - 1)
            def _():
                pack(number + 1, block, parity, links)
                for side, target in ((0, left), (1, right)):
                    halo(number + 1, block, side, target).start()

    def send_loops(sweep, parity):
        low = shifts.low_rows
        number = 2 * sweep + parity
        even, uneven = [], []
        for entry in range(18):
            a = field[parity, entry, pl.ds(0, 8), :]
            b = field[parity, entry, pl.ds(4, 8), :]
            c = field[parity, entry, pl.ds(8, 8), :]
            even.append(jnp.where(low, a, b))
            uneven.append(jnp.where(low, b, c))
        re, im = times(split(even), split(uneven))
        re, im = times((re, im), ([turn_rows(v, 4) for v in re], [turn_rows(v, 4) for v in im]))
        for entry, value in enumerate(re + im):
            loop_rows[pl.ds(8 * entry, 8), :] = value
        for j in range(3):
            for third in range(3):
                loop_out[number, j, pl.ds(8 * third, 8), :] = (
                    loop_rows[pl.ds(64 * third + j, 8, stride=8), :])

        def loop_to(peer_x):
            at = pl.multiple_of(24 * (2 * ix + parity), 8)
            return (
                loop_out.at[number, peer_x - 1, pl.ds(0, 18), :],
                loop_in.at[sweep, iz, pl.ds(at, 18), :])

        for step in range(nx * nz):
            if step == 0:
                @pl.when(ix > 0)
                def _():
                    pltpu.make_async_copy(*loop_to(ix), local_sem.at[number]).start()
            else:
                peer = lax.rem(slab + step, nx * nz)
                peer_x, peer_z = peer // nz, lax.rem(peer, nz)

                @pl.when(peer_x > 0)
                def _():
                    remote(
                        *loop_to(peer_x), loop_sent.at[number], loop_got.at[number],
                        (peer_x, peer_z, ia)).start()

    @pl.loop(0, SWEEPS)
    def _(sweep):
        for parity in (0, 1):
            half_sweep(sweep, parity)
            send_loops(sweep, parity)

    def normalized(load, store, log):
        square = None
        for k in range(162):
            value = load(k)
            square = value * value if square is None else square + value * value
        rms = jnp.sqrt(square / 162.0 + 1e-06)
        inv = 1.0 / rms
        for k in range(162):
            store(k, load(k) * inv)
        return log + jnp.log(rms)

    def combine(left_ref, right_ref, dst_ref, keep):
        @pl.loop(0, 9)
        def _(row):
            for half in range(3):
                columns = range(3 * half, 3 * half + 3)
                re, im = [None] * 3, [None] * 3
                for mid in range(9):
                    a_re, a_im = left_ref[9 * row + mid], left_ref[81 + 9 * row + mid]
                    for place, col in enumerate(columns):
                        b_re, b_im = right_ref[9 * mid + col], right_ref[81 + 9 * mid + col]
                        p_re = a_re * b_re - a_im * b_im
                        p_im = a_re * b_im + a_im * b_re
                        re[place] = p_re if re[place] is None else re[place] + p_re
                        im[place] = p_im if im[place] is None else im[place] + p_im
                for place, col in enumerate(columns):
                    dst_ref[9 * row + col] = re[place]
                    dst_ref[81 + 9 * row + col] = im[place]
        log = normalized(
            lambda k: dst_ref[k], lambda k, value: dst_ref.__setitem__(k, keep(k, value)),
            left_ref[162] + right_ref[162])
        dst_ref[162] = keep(162, log)

    def result_to(target):
        lanes = pl.ds(pl.multiple_of(LANES * (ix - 1), LANES), LANES)
        rows = pl.ds(2 * target, 2)
        return (
            (final.at[pl.ds(0, 162), rows, :], out_hbm.at[:, :, lanes]),
            (final.at[162, rows, :], log_hbm.at[:, lanes]))

    @pl.when(ix > 0)
    def _():
        for number in range(halves):
            ref = loop_out.at[number, 0, pl.ds(0, 18), :]
            landed(ref, local_sem.at[number])
            landed(space_raw.at[0, :, pl.ds(0, 15), :], loop_got.at[number])

        @pl.loop(0, nz)
        def _(slot):
            for sweep in range(SWEEPS):
                loops = [loop_in[sweep, slot, pl.ds(k, 8, stride=24), :] for k in range(18)]
                partner = [shifts.deep(value, 4) for value in loops]
                for a in range(3):
                    for c in range(3):
                        for e in range(3):
                            for d in range(3):
                                l_re, l_im = loops[3 * a + e], loops[9 + 3 * a + e]
                                r_re, r_im = partner[3 * c + d], partner[9 + 3 * c + d]
                                re = l_re * r_re + l_im * r_im
                                im = l_im * r_re - l_re * r_im
                                at = 9 * (3 * a + c) + 3 * e + d
                                if sweep:
                                    re = oper[slot, at] + re
                                    im = oper[slot, 81 + at] + im
                                oper[slot, at] = re
                                oper[slot, 81 + at] = im
            third = 1.0 / SWEEPS
            log = normalized(
                lambda k: oper[slot, k] * third,
                lambda k, value: oper.at[slot].__setitem__(k, value), jnp.zeros((8, LANES)))
            oper[slot, 162] = log

        @pl.loop(0, 163)
        def _(k):
            part[0, k] = oper[0, k]

        @pl.loop(1, nz)
        def _(slot):
            combine(part.at[slot - 1], oper.at[slot], part.at[slot], lambda k, value: value)

        row = lax.broadcasted_iota(jnp.int32, (8, LANES), 0)

        def moved(value, k, rows):
            unit = 1.0 if k < 81 and k % 10 == 0 else 0.0
            return jnp.where(row < rows, unit, turn_rows(value, -rows))

        def by_column(k, value):
            swapped = jnp.where(row % 2 == 0, turn_rows(value, 1), turn_rows(value, -1))
            return jnp.where(odd, swapped, value)

        for k in range(163):
            chain_a[k] = moved(part[nz - 1, k], k, 2)
            chain_b[k] = moved(chain_a[k], k, 2)
        combine(chain_b, chain_a, group, lambda k, value: jnp.where(row < 2, chain_a[k], value))
        for k in range(163):
            chain_b[k] = moved(group[k], k, 4)
        combine(chain_b, group, chain_a, lambda k, value: jnp.where(row < 4, group[k], value))
        combine(chain_a, part.at[iz], final, by_column)

        for target in range(nx):
            @pl.when(ix == target)
            def _():
                for piece, (src, dst) in enumerate(result_to(target)):
                    pltpu.make_async_copy(src, dst, done_sem.at[piece]).start()

            @pl.when(ix != target)
            def _():
                for piece, (src, dst) in enumerate(result_to(target)):
                    remote(
                        src, dst, done_sem.at[2 + piece], back_sem.at[piece, ix], (target, iz, ia)
                    ).start()
        for piece, (src, dst) in enumerate(result_to(0)):
            pltpu.make_async_copy(src, dst, done_sem.at[piece]).wait()

    for source in range(1, nx):
        @pl.when(ix != source)
        def _():
            landed(final.at[pl.ds(0, 162), pl.ds(0, 2), :], back_sem.at[0, source])
            landed(final.at[162, pl.ds(0, 2), :], back_sem.at[1, source])

    for copy in edges:
        copy.wait_send()
    for number in range(halves):
        for block in range(2):
            for side in range(2):
                halo(number, block, side, left).wait_send()

    @pl.when(ix == 0)
    def _():
        for number in range(halves):
            landed(space_raw.at[0, :, pl.ds(0, 12), :], loop_sent.at[number])

    @pl.when(ix > 0)
    def _():
        for number in range(halves):
            landed(space_raw.at[0, :, pl.ds(0, 11), :], loop_sent.at[number])
        landed(final.at[pl.ds(0, 162), pl.ds(0, 6), :], done_sem.at[2])
        landed(final.at[162, pl.ds(0, 6), :], done_sem.at[3])


def per_device(temporal_links, spatial_links, rotations):
    f32, dma = jnp.float32, pltpu.SemaphoreType.DMA
    halves = 2 * SWEEPS
    transfer, log_scale = pl.pallas_call(
        kernel,
        name="slab_chain",
        out_shape=(
            jax.ShapeDtypeStruct((162, 2, 3 * LANES), f32),
            jax.ShapeDtypeStruct((2, 3 * LANES), f32),
        ),
        in_specs=[pl.BlockSpec(memory_space=pl.ANY)] * 3,
        out_specs=[pl.BlockSpec(memory_space=pl.ANY)] * 2,
        scratch_shapes=[
            pltpu.VMEM((18, 32, LANES), f32),
            pltpu.VMEM((3, 18, 48, LANES), f32),
            pltpu.VMEM((3, 3, 4, 32, LANES), f32),
            pltpu.VMEM((12, 16, LANES), f32),
            pltpu.VMEM((12, 16, LANES), f32),
            pltpu.VMEM((12, 16, LANES), f32),
            pltpu.VMEM((2, 18, 16, LANES), f32),
            pltpu.VMEM((2, 6, 18, 24, LANES), f32),
            pltpu.VMEM((4, 18, 8, LANES), f32),
            pltpu.VMEM((halves, 2, 2, 9, 8, LANES), f32),
            pltpu.VMEM((halves, 2, 2, 9, 8, LANES), f32),
            pltpu.VMEM((192, LANES), f32),
            pltpu.VMEM((halves, 3, 24, LANES), f32),
            pltpu.VMEM((SWEEPS, 4, 192, LANES), f32),
            pltpu.VMEM((4, 163, 8, LANES), f32),
            pltpu.VMEM((163, 8, LANES), f32),
            pltpu.VMEM((163, 8, LANES), f32),
            pltpu.VMEM((163, 8, LANES), f32),
            pltpu.VMEM((4, 163, 8, LANES), f32),
            pltpu.VMEM((163, 8, LANES), f32),
            dma((3,)), dma((5,)), dma((5,)), dma((halves, 2, 2)), dma((halves, 2, 2)),
            dma((halves,)), dma((halves,)), dma((halves,)), dma((2, 4)), dma((4,)),
        ],
        compiler_params=pltpu.CompilerParams(collective_id=0, has_side_effects=True),
    )(temporal_links, spatial_links, rotations)
    return transfer.reshape(2, 9, 9, 1, 2, 3 * LANES), log_scale.reshape(1, 2, 3 * LANES)


def solution(mesh):
    split = Mesh(mesh.devices.reshape(4, 4, mesh.shape["sa"]), AXES)
    slabs = ("ta_0", "ta_1")
    return jax.shard_map(
        per_device,
        mesh=split,
        in_specs=(
            P(None, slabs, "sa", None),
            P(None, None, slabs, "sa", None),
            P(None, None, None, slabs, "sa", None),
        ),
        out_specs=(P(None, None, None, slabs, "sa", None), P(slabs, "sa", None)),
        check_vma=False,
    )
```

time: 79.9 us -> 73.7 us (0.922)
  Pallas kernels: 74.2 us -> 69.7 us
  local copies, waits for them, and re-layouts: 3.66 us -> 2.57 us
    pallas_call x1, Pallas kernels: 74.2 us -> 69.7 us  [per_device(): pl.pallas_call(kernel, name='slab_chain', out_shape=(jax.ShapeDtypeStruct...]
    reshape x3 -> x0, local copies, waits for them, and re-layouts: 2.63 us -> none  [the longest x1 1.24 us: per_device(): log_scale = out[162].transpose(1, 0, 2).reshape(1, 2, 3 * LANES)]
    unnamed x0 -> x4, local copies, waits for them, and re-layouts: none -> 2.57 us
    slice x2 -> x0, local copies, waits for them, and re-layouts: 1.03 us -> none  [per_device(): out[:162].reshape(2, 9, 9, 3, 2, LANES).transpose(0, 1, 2, 4, 3, 5)]
where the time goes in v1:
time: 73.7 us; the launch traced here: 72.9 us
  Pallas kernels  69.7 us (95%)
  local copies, waits for them, and re-layouts  2.57 us (3%)
    pallas_call x1, Pallas kernels, per_device(): pl.pallas_call(kernel, name='slab_chain', out_shape=(jax.ShapeDtypeStruct...  69.7 us
    unnamed x4, local copies, waits for them, and re-layouts  2.57 us

profile of v1, /device:TPU:6, one launch (start us, length us, event | category | flops | bytes accessed | tf_op | source)
XLA Modules:
  0.0 72.9 jit_solution(17383650771089669826)
XLA Ops:
  0.6 69.7 %slab_chain.1 = (f32[162,2,384]{2,1,0:T(2,128)}, f32[2,384]{1,0:T(2,128)}) custom-call(f32[18,4,2,384]{3,2,1,0:T(2,128)} %time_hbm.1, f32[3,18,4,2,384]{4,3,2,1,0:T(2,128)} %space_hbm.1, f32[3,3,4,4,2,384]{5,4,3,2,1,0:T(2,128)} %turn_hbm.1), custom_call_target="tpu_custom_call" | custom-call | tf_op jit(solution)/shard_map/slab_chain/pallas_call | solution.py:567
  70.3 0.0 copy-start
  70.3 2.0 %copy.8 = f32[2,9,9,1,2,384]{5,4,3,2,1,0:T(2,128)} copy(f32[2,9,9,1,2,384]{5,4,3,2,1,0:T(2,128)} %bitcast.4) | data formatting | bytes 995328
  72.3 0.0 copy-done
  72.3 0.6 copy.9
Async XLA Ops:
  70.3 2.0 %copy-start = (f32[2,384]{1,0:T(2,128)S(1)}, f32[2,384]{1,0:T(2,128)}, u32[]{:S(2)}) copy-start(f32[2,384]{1,0:T(2,128)} %get-tuple-element.5) | copy-start | bytes 9220

commit v2 on v1

--- a/solution.py
+++ b/solution.py
@@ -153,7 +153,7 @@
     time_hbm, space_hbm, turn_hbm, out_hbm, log_hbm,
     time_raw, space_raw, turn_raw, left_out, left_in, left_next,
     field, bonds, shifted, pack_out, pack_in, loop_rows, loop_out, loop_in,
-    oper, chain_a, chain_b, group, part, final,
+    oper, chain_a, chain_b, group, sums, final,
     in_sem, edge_out, edge_in, halo_out, halo_in, loop_sent, loop_got, local_sem, back_sem, done_sem,
 ):
     ix, iz, ia = lax.axis_index("ta_0"), lax.axis_index("ta_1"), lax.axis_index("sa")
@@ -213,11 +213,24 @@
             pack_out[number, block, 0, k] = own(parity, real, partner)
             pack_out[number, block, 1, k] = own(parity, partner, real)
 
-    def halo(number, block, side, target):
-        return remote(
-            pack_out.at[number, block, side], pack_in.at[number, block, side],
-            halo_out.at[number, block, side], halo_in.at[number, block, side], (ix, iz, target))
-
+    def send_halo(number, block, side, target):
+        for at in (0, 4):
+            rows = pl.ds(at, 3)
+            remote(
+                pack_out.at[number, block, side, :, rows, :],
+                pack_in.at[number, block, side, :, rows, :],
+                halo_out.at[number, block, side], halo_in.at[number, block, side],
+                (ix, iz, target)).start()
+
+    def await_halo(sem, number, block, side):
+        landed(pack_in.at[number, block, side, :, pl.ds(0, 6), :], sem.at[number, block, side])
+
+    two_rows = [*range(6), *range(9, 15)]
+    landed(space_raw.at[:, :, pl.ds(0, 24), :], in_sem.at[1])
+    for block in range(2):
+        for place, entry in enumerate(two_rows):
+            left_out[place, pl.ds(8 * block, 8), :] = (
+                space_raw[0, entry, pl.ds(16 * block + 1, 8, stride=2), :])
     landed(time_raw.at[:, pl.ds(0, 24), :], in_sem.at[0])
     for block in range(2):
         packed = []
@@ -229,12 +242,30 @@
             field[1, entry, pl.ds(8 * block, 8), :] = value
             packed.append(value)
         pack(0, block, 1, split(packed))
-    landed(space_raw.at[:, :, pl.ds(0, 24), :], in_sem.at[1])
-    two_rows = [*range(6), *range(9, 15)]
+    pl.semaphore_wait(barrier, len(peers))
     for block in range(2):
-        for place, entry in enumerate(two_rows):
-            left_out[place, pl.ds(8 * block, 8), :] = (
-                space_raw[0, entry, pl.ds(16 * block + 1, 8, stride=2), :])
+        for side, target in ((0, left), (1, right)):
+            send_halo(0, block, side, target)
+    edges = []
+    for t in range(4):
+        rows = pl.ds(4 * t, 3)
+        edges.append(remote(
+            left_out.at[:, rows, :], left_in.at[:, rows, :], edge_out.at[0], edge_in.at[0],
+            (ix, iz, right)))
+    for half in range(2):
+        rows = pl.ds(0, 6)
+        edges.append(remote(
+            space_raw.at[:, pl.ds(9 * half, 6), rows, :],
+            space_raw.at[:, pl.ds(9 * half, 6), pl.ds(32, 6), :],
+            edge_out.at[1 + half], edge_in.at[1 + half], (earlier_x, earlier_z, ia)))
+    edges.append(remote(
+        left_out.at[:, pl.ds(0, 3), :], left_next.at[:, pl.ds(0, 3), :],
+        edge_out.at[3], edge_in.at[3], (earlier_x, earlier_z, right)))
+    for copy in edges:
+        copy.start()
+    covers = (
+        left_in.at[:, pl.ds(0, 12), :], space_raw.at[:, pl.ds(0, 6), pl.ds(0, 6), :],
+        space_raw.at[:, pl.ds(0, 6), pl.ds(0, 6), :], left_in.at[:, pl.ds(0, 3), :])
 
     def raw(direction, at, column):
         return [space_raw[direction, k, pl.ds(at + column, 8, stride=2), :] for k in range(18)]
@@ -268,7 +299,7 @@
         if block < 2:
             six = [left_in[k, to, :] for k in range(12)]
         else:
-            six = [left_next[k, pl.ds(1, 8, stride=2), :] for k in range(12)]
+            six = [left_next[k] for k in range(12)]
         beyond = dagger(closed((six[:6], six[6:])))
         beyond = beyond[0] + beyond[1]
         for parity in (0, 1):
@@ -279,25 +310,8 @@
     def _(block):
         inner_bonds(block)
 
-    pl.semaphore_wait(barrier, len(peers))
-    for block in range(2):
-        for side, target in ((0, left), (1, right)):
-            halo(0, block, side, target).start()
-    edges = [remote(left_out, left_in, edge_out.at[0], edge_in.at[0], (ix, iz, right))]
-    for half in range(2):
-        rows = pl.ds(0, 6)
-        edges.append(remote(
-            space_raw.at[:, pl.ds(9 * half, 6), rows, :],
-            space_raw.at[:, pl.ds(9 * half, 6), pl.ds(32, 6), :],
-            edge_out.at[1 + half], edge_in.at[1 + half], (earlier_x, earlier_z, ia)))
-        edges.append(remote(
-            space_raw.at[0, pl.ds(9 * half, 6), rows, :],
-            left_next.at[pl.ds(6 * half, 6), rows, :],
-            edge_out.at[3 + half], edge_in.at[3 + half], (earlier_x, earlier_z, right)))
-    for copy in edges:
-        copy.start()
     landed(turn_raw.at[:, :, :, pl.ds(0, 24), :], in_sem.at[2])
-    edges[0].wait_recv()
+    landed(covers[0], edge_in.at[0])
     for block in range(2):
         outer_bonds(block)
 
@@ -312,8 +326,8 @@
             if parity == 0:
                 @pl.when(jnp.logical_and(sweep == 0, block == 1))
                 def _():
-                    for copy in edges[1:]:
-                        copy.wait_recv()
+                    for piece in range(1, 4):
+                        landed(covers[piece], edge_in.at[piece])
                     for direction in range(3):
                         six = [space_raw[direction, k, pl.ds(32, 8), :] for k in two_rows]
                         re, im = closed((six[:6], six[6:]))
@@ -343,7 +357,7 @@
                     load(shifted, (place - 1,), slice(None)))
 
             for side in range(2):
-                halo(number, block, side, left).wait_recv()
+                await_halo(halo_in, number, block, side)
             beyond_re, beyond_im = [], []
             for k in range(9):
                 from_left = pack_in[number, block, 1, k]
@@ -373,7 +387,7 @@
             def _():
                 pack(number + 1, block, parity, links)
                 for side, target in ((0, left), (1, right)):
-                    halo(number + 1, block, side, target).start()
+                    send_halo(number + 1, block, side, target)
 
     def send_loops(sweep, parity):
         low = shifts.low_rows
@@ -433,22 +447,27 @@
         return log + jnp.log(rms)
 
     def combine(left_ref, right_ref, dst_ref, keep):
+        for k in range(81):
+            sums[k] = right_ref[k] + right_ref[81 + k]
+
         @pl.loop(0, 9)
         def _(row):
-            for half in range(3):
-                columns = range(3 * half, 3 * half + 3)
-                re, im = [None] * 3, [None] * 3
+            for third in range(3):
+                columns = range(3 * third, 3 * third + 3)
+                acc = [[None] * 3 for _ in columns]
                 for mid in range(9):
                     a_re, a_im = left_ref[9 * row + mid], left_ref[81 + 9 * row + mid]
+                    a_sum = a_re + a_im
                     for place, col in enumerate(columns):
-                        b_re, b_im = right_ref[9 * mid + col], right_ref[81 + 9 * mid + col]
-                        p_re = a_re * b_re - a_im * b_im
-                        p_im = a_re * b_im + a_im * b_re
-                        re[place] = p_re if re[place] is None else re[place] + p_re
-                        im[place] = p_im if im[place] is None else im[place] + p_im
+                        at = 9 * mid + col
+                        terms = (a_re * right_ref[at], a_im * right_ref[81 + at], a_sum * sums[at])
+                        for slot, term in enumerate(terms):
+                            old = acc[place][slot]
+                            acc[place][slot] = term if old is None else old + term
                 for place, col in enumerate(columns):
-                    dst_ref[9 * row + col] = re[place]
-                    dst_ref[81 + 9 * row + col] = im[place]
+                    plain, cross, both = acc[place]
+                    dst_ref[9 * row + col] = plain - cross
+                    dst_ref[81 + 9 * row + col] = both - plain - cross
         log = normalized(
             lambda k: dst_ref[k], lambda k, value: dst_ref.__setitem__(k, keep(k, value)),
             left_ref[162] + right_ref[162])
@@ -463,43 +482,49 @@
 
     @pl.when(ix > 0)
     def _():
-        for number in range(halves):
+        def await_loops(number):
             ref = loop_out.at[number, 0, pl.ds(0, 18), :]
             landed(ref, local_sem.at[number])
             landed(space_raw.at[0, :, pl.ds(0, 15), :], loop_got.at[number])
 
-        @pl.loop(0, nz)
-        def _(slot):
-            for sweep in range(SWEEPS):
-                loops = [loop_in[sweep, slot, pl.ds(k, 8, stride=24), :] for k in range(18)]
-                partner = [shifts.deep(value, 4) for value in loops]
-                for a in range(3):
-                    for c in range(3):
-                        for e in range(3):
-                            for d in range(3):
-                                l_re, l_im = loops[3 * a + e], loops[9 + 3 * a + e]
-                                r_re, r_im = partner[3 * c + d], partner[9 + 3 * c + d]
-                                re = l_re * r_re + l_im * r_im
-                                im = l_im * r_re - l_re * r_im
-                                at = 9 * (3 * a + c) + 3 * e + d
-                                if sweep:
-                                    re = oper[slot, at] + re
-                                    im = oper[slot, 81 + at] + im
-                                oper[slot, at] = re
-                                oper[slot, 81 + at] = im
-            third = 1.0 / SWEEPS
-            log = normalized(
-                lambda k: oper[slot, k] * third,
-                lambda k, value: oper.at[slot].__setitem__(k, value), jnp.zeros((8, LANES)))
-            oper[slot, 162] = log
-
-        @pl.loop(0, 163)
-        def _(k):
-            part[0, k] = oper[0, k]
+        def add_operator(slot, sweep):
+            to = jnp.where(slot == 0, 0, slot + 3)
+            loops = [loop_in[sweep, slot, pl.ds(k, 8, stride=24), :] for k in range(18)]
+            partner = [shifts.deep(value, 4) for value in loops]
+            for a in range(3):
+                for c in range(3):
+                    for e in range(3):
+                        for d in range(3):
+                            l_re, l_im = loops[3 * a + e], loops[9 + 3 * a + e]
+                            r_re, r_im = partner[3 * c + d], partner[9 + 3 * c + d]
+                            re = l_re * r_re + l_im * r_im
+                            im = l_im * r_re - l_re * r_im
+                            at = 9 * (3 * a + c) + 3 * e + d
+                            if sweep:
+                                re = oper[to, at] + re
+                                im = oper[to, 81 + at] + im
+                            oper[to, at] = re
+                            oper[to, 81 + at] = im
+            return to
+
+        for sweep in range(SWEEPS):
+            await_loops(2 * sweep)
+            await_loops(2 * sweep + 1)
+
+            @pl.loop(0, nz)
+            def _(slot):
+                to = add_operator(slot, sweep)
+                if sweep == SWEEPS - 1:
+                    third = 1.0 / SWEEPS
+                    log = normalized(
+                        lambda k: oper[to, k] * third,
+                        lambda k, value: oper.at[to].__setitem__(k, value),
+                        jnp.zeros((8, LANES)))
+                    oper[to, 162] = log
 
         @pl.loop(1, nz)
         def _(slot):
-            combine(part.at[slot - 1], oper.at[slot], part.at[slot], lambda k, value: value)
+            combine(oper.at[slot - 1], oper.at[slot + 3], oper.at[slot], lambda k, value: value)
 
         row = lax.broadcasted_iota(jnp.int32, (8, LANES), 0)
 
@@ -512,13 +537,13 @@
             return jnp.where(odd, swapped, value)
 
         for k in range(163):
-            chain_a[k] = moved(part[nz - 1, k], k, 2)
+            chain_a[k] = moved(oper[nz - 1, k], k, 2)
             chain_b[k] = moved(chain_a[k], k, 2)
         combine(chain_b, chain_a, group, lambda k, value: jnp.where(row < 2, chain_a[k], value))
         for k in range(163):
             chain_b[k] = moved(group[k], k, 4)
         combine(chain_b, group, chain_a, lambda k, value: jnp.where(row < 4, group[k], value))
-        combine(chain_a, part.at[iz], final, by_column)
+        combine(chain_a, oper.at[iz], final, by_column)
 
         for target in range(nx):
             @pl.when(ix == target)
@@ -541,12 +566,12 @@
             landed(final.at[pl.ds(0, 162), pl.ds(0, 2), :], back_sem.at[0, source])
             landed(final.at[162, pl.ds(0, 2), :], back_sem.at[1, source])
 
-    for copy in edges:
-        copy.wait_send()
+    for piece, cover in enumerate(covers):
+        landed(cover, edge_out.at[piece])
     for number in range(halves):
         for block in range(2):
             for side in range(2):
-                halo(number, block, side, left).wait_send()
+                await_halo(halo_out, number, block, side)
 
     @pl.when(ix == 0)
     def _():
@@ -559,6 +584,24 @@
             landed(space_raw.at[0, :, pl.ds(0, 11), :], loop_sent.at[number])
         landed(final.at[pl.ds(0, 162), pl.ds(0, 6), :], done_sem.at[2])
         landed(final.at[162, pl.ds(0, 6), :], done_sem.at[3])
+
+
+def finish(transfer_in, log_in, transfer_out, log_out, held, log_held, sem_in, sem_out):
+    pieces = [
+        (transfer_in.at[pl.ds(27 * k, 27)], held.at[pl.ds(27 * k, 27)],
+         transfer_out.at[pl.ds(27 * k, 27)])
+        for k in range(6)
+    ] + [(log_in, log_held, log_out)]
+    ins = [pltpu.make_async_copy(src, mid, sem_in.at[k]) for k, (src, mid, _) in enumerate(pieces)]
+    outs = [
+        pltpu.make_async_copy(mid, dst, sem_out.at[k]) for k, (_, mid, dst) in enumerate(pieces)]
+    for copy in ins:
+        copy.start()
+    for arrived, leaving in zip(ins, outs):
+        arrived.wait()
+        leaving.start()
+    for copy in outs:
+        copy.wait()
 
 
 def per_device(temporal_links, spatial_links, rotations):
@@ -579,7 +622,7 @@
             pltpu.VMEM((3, 3, 4, 32, LANES), f32),
             pltpu.VMEM((12, 16, LANES), f32),
             pltpu.VMEM((12, 16, LANES), f32),
-            pltpu.VMEM((12, 16, LANES), f32),
+            pltpu.VMEM((12, 8, LANES), f32),
             pltpu.VMEM((2, 18, 16, LANES), f32),
             pltpu.VMEM((2, 6, 18, 24, LANES), f32),
             pltpu.VMEM((4, 18, 8, LANES), f32),
@@ -588,17 +631,31 @@
             pltpu.VMEM((192, LANES), f32),
             pltpu.VMEM((halves, 3, 24, LANES), f32),
             pltpu.VMEM((SWEEPS, 4, 192, LANES), f32),
-            pltpu.VMEM((4, 163, 8, LANES), f32),
+            pltpu.VMEM((7, 163, 8, LANES), f32),
             pltpu.VMEM((163, 8, LANES), f32),
             pltpu.VMEM((163, 8, LANES), f32),
             pltpu.VMEM((163, 8, LANES), f32),
-            pltpu.VMEM((4, 163, 8, LANES), f32),
+            pltpu.VMEM((81, 8, LANES), f32),
             pltpu.VMEM((163, 8, LANES), f32),
-            dma((3,)), dma((5,)), dma((5,)), dma((halves, 2, 2)), dma((halves, 2, 2)),
+            dma((3,)), dma((4,)), dma((4,)), dma((halves, 2, 2)), dma((halves, 2, 2)),
             dma((halves,)), dma((halves,)), dma((halves,)), dma((2, 4)), dma((4,)),
         ],
         compiler_params=pltpu.CompilerParams(collective_id=0, has_side_effects=True),
     )(temporal_links, spatial_links, rotations)
+    transfer, log_scale = pl.pallas_call(
+        finish,
+        name="hand_over",
+        out_shape=(
+            jax.ShapeDtypeStruct((162, 2, 3 * LANES), f32),
+            jax.ShapeDtypeStruct((2, 3 * LANES), f32),
+        ),
+        in_specs=[pl.BlockSpec(memory_space=pl.ANY)] * 2,
+        out_specs=[pl.BlockSpec(memory_space=pl.ANY)] * 2,
+        scratch_shapes=[
+            pltpu.VMEM((162, 2, 3 * LANES), f32), pltpu.VMEM((2, 3 * LANES), f32),
+            dma((7,)), dma((7,)),
+        ],
+    )(transfer, log_scale)
     return transfer.reshape(2, 9, 9, 1, 2, 3 * LANES), log_scale.reshape(1, 2, 3 * LANES)
 
 

time: 73.7 us -> 67.7 us (0.919)
  Pallas kernels: 69.7 us -> 66.9 us
  local copies, waits for them, and re-layouts: 2.57 us -> 0 us
    pallas_call x1, Pallas kernels: 69.7 us -> 65 us  [per_device(): pl.pallas_call(kernel, name='slab_chain', out_shape=(jax.ShapeDtypeStruct...]
    unnamed x4 -> x0, local copies, waits for them, and re-layouts: 2.57 us -> none
    pallas_call x0 -> x1, Pallas kernels: none -> 1.85 us  [per_device(): pl.pallas_call(finish, name='hand_over', out_shape=(jax.ShapeDtypeStruct(...]
where the time goes in v2:
time: 67.7 us; the launch traced here: 67.5 us
  Pallas kernels  66.9 us (99%)
    pallas_call x1, Pallas kernels, per_device(): pl.pallas_call(kernel, name='slab_chain', out_shape=(jax.ShapeDtypeStruct...  65 us
    pallas_call x1, Pallas kernels, per_device(): pl.pallas_call(finish, name='hand_over', out_shape=(jax.ShapeDtypeStruct(...  1.85 us

profile of v2, /device:TPU:6, one launch (start us, length us, event | category | flops | bytes accessed | tf_op | source)
XLA Modules:
  0.0 67.5 jit_solution(9322066455047429480)
XLA Ops:
  0.6 65.0 %slab_chain.1 = (f32[162,2,384]{2,1,0:T(2,128)}, f32[2,384]{1,0:T(2,128)}) custom-call(f32[18,4,2,384]{3,2,1,0:T(2,128)} %time_hbm.1, f32[3,18,4,2,384]{4,3,2,1,0:T(2,128)} %space_hbm.1, f32[3,3,4,4,2,384]{5,4,3,2,1,0:T(2,128)} %turn_hbm.1), custom_call_target="tpu_custom_call" | custom-call | tf_op jit(solution)/shard_map/slab_chain/pallas_call | solution.py:610
  65.7 1.8 %hand_over.1 = (f32[162,2,384]{2,1,0:T(2,128)}, f32[2,384]{1,0:T(2,128)}) custom-call(f32[162,2,384]{2,1,0:T(2,128)} %get-tuple-element.6.transfer_in, f32[2,384]{1,0:T(2,128)} %get-tuple-element.7.log_in), custom_call_target="tpu_custom_call" | custom-call | tf_op jit(solution)/shard_map/hand_over/pallas_call | solution.py:645

commit v3 on v2

--- a/solution.py
+++ b/solution.py
@@ -155,6 +155,7 @@
     field, bonds, shifted, pack_out, pack_in, loop_rows, loop_out, loop_in,
     oper, chain_a, chain_b, group, sums, final,
     in_sem, edge_out, edge_in, halo_out, halo_in, loop_sent, loop_got, local_sem, back_sem, done_sem,
+    known,
 ):
     ix, iz, ia = lax.axis_index("ta_0"), lax.axis_index("ta_1"), lax.axis_index("sa")
     nx, nz, na = 4, 4, lax.axis_size("sa")
@@ -181,11 +182,8 @@
             ).start()
 
     barrier = pltpu.get_barrier_semaphore()
-    peers = []
-    for step in range(1, nx * nz):
-        peer = lax.rem(slab + step, nx * nz)
-        peers.append((peer // nz, lax.rem(peer, nz), ia))
-    peers += [(ix, iz, left), (ix, iz, right)]
+    peers = [(ix, iz, left), (ix, iz, right)]
+    peers += [(earlier_x, earlier_z, ia), (later_x, later_z, ia)]
     peers += [(earlier_x, earlier_z, right), (later_x, later_z, left)]
     for peer in peers:
         pl.semaphore_signal(barrier, inc=1, device_id=peer, device_id_type=MESH)
@@ -197,6 +195,17 @@
 
     def landed(ref, sem):
         pltpu.make_async_copy(ref, ref, sem).wait()
+
+    def tell(stage):
+        for side, step in ((0, 1 << stage), (1, nx * nz - (1 << stage))):
+            peer = lax.rem(slab + step, nx * nz)
+            pl.semaphore_signal(
+                known.at[stage, side], inc=1, device_id=(peer // nz, lax.rem(peer, nz), ia),
+                device_id_type=MESH)
+
+    def hear(stage):
+        for side in range(2):
+            pl.semaphore_wait(known.at[stage, side], 1)
 
     shifts = Shifts()
     odd = shifts.odd
@@ -263,6 +272,7 @@
         edge_out.at[3], edge_in.at[3], (earlier_x, earlier_z, right)))
     for copy in edges:
         copy.start()
+    tell(0)
     covers = (
         left_in.at[:, pl.ds(0, 12), :], space_raw.at[:, pl.ds(0, 6), pl.ds(0, 6), :],
         space_raw.at[:, pl.ds(0, 6), pl.ds(0, 6), :], left_in.at[:, pl.ds(0, 3), :])
@@ -314,6 +324,8 @@
     landed(covers[0], edge_in.at[0])
     for block in range(2):
         outer_bonds(block)
+    hear(0)
+    tell(1)
 
     def half_sweep(sweep, parity):
         number = 2 * sweep + parity
@@ -328,6 +340,8 @@
                 def _():
                     for piece in range(1, 4):
                         landed(covers[piece], edge_in.at[piece])
+                    hear(1)
+                    tell(2)
                     for direction in range(3):
                         six = [space_raw[direction, k, pl.ds(32, 8), :] for k in two_rows]
                         re, im = closed((six[:6], six[6:]))
@@ -414,14 +428,13 @@
                 loop_out.at[number, peer_x - 1, pl.ds(0, 18), :],
                 loop_in.at[sweep, iz, pl.ds(at, 18), :])
 
-        for step in range(nx * nz):
-            if step == 0:
+        for step_z, step_x in [(z, x) for z in (2, 1, 3, 0) for x in (2, 1, 3, 0)]:
+            if step_z == step_x == 0:
                 @pl.when(ix > 0)
                 def _():
                     pltpu.make_async_copy(*loop_to(ix), local_sem.at[number]).start()
             else:
-                peer = lax.rem(slab + step, nx * nz)
-                peer_x, peer_z = peer // nz, lax.rem(peer, nz)
+                peer_x, peer_z = lax.rem(ix + step_x, nx), lax.rem(iz + step_z, nz)
 
                 @pl.when(peer_x > 0)
                 def _():
@@ -433,6 +446,10 @@
     def _(sweep):
         for parity in (0, 1):
             half_sweep(sweep, parity)
+            if parity == 0:
+                @pl.when(sweep == 0)
+                def _():
+                    hear(2)
             send_loops(sweep, parity)
 
     def normalized(load, store, log):
@@ -586,36 +603,15 @@
         landed(final.at[162, pl.ds(0, 6), :], done_sem.at[3])
 
 
-def finish(transfer_in, log_in, transfer_out, log_out, held, log_held, sem_in, sem_out):
-    pieces = [
-        (transfer_in.at[pl.ds(27 * k, 27)], held.at[pl.ds(27 * k, 27)],
-         transfer_out.at[pl.ds(27 * k, 27)])
-        for k in range(6)
-    ] + [(log_in, log_held, log_out)]
-    ins = [pltpu.make_async_copy(src, mid, sem_in.at[k]) for k, (src, mid, _) in enumerate(pieces)]
-    outs = [
-        pltpu.make_async_copy(mid, dst, sem_out.at[k]) for k, (_, mid, dst) in enumerate(pieces)]
-    for copy in ins:
-        copy.start()
-    for arrived, leaving in zip(ins, outs):
-        arrived.wait()
-        leaving.start()
-    for copy in outs:
-        copy.wait()
-
-
 def per_device(temporal_links, spatial_links, rotations):
     f32, dma = jnp.float32, pltpu.SemaphoreType.DMA
     halves = 2 * SWEEPS
     transfer, log_scale = pl.pallas_call(
         kernel,
         name="slab_chain",
-        out_shape=(
-            jax.ShapeDtypeStruct((162, 2, 3 * LANES), f32),
-            jax.ShapeDtypeStruct((2, 3 * LANES), f32),
-        ),
+        out_shape=(pltpu.VMEM((162, 2, 3 * LANES), f32), pltpu.VMEM((2, 3 * LANES), f32)),
         in_specs=[pl.BlockSpec(memory_space=pl.ANY)] * 3,
-        out_specs=[pl.BlockSpec(memory_space=pl.ANY)] * 2,
+        out_specs=[pl.BlockSpec(memory_space=pltpu.VMEM)] * 2,
         scratch_shapes=[
             pltpu.VMEM((18, 32, LANES), f32),
             pltpu.VMEM((3, 18, 48, LANES), f32),
@@ -639,23 +635,10 @@
             pltpu.VMEM((163, 8, LANES), f32),
             dma((3,)), dma((4,)), dma((4,)), dma((halves, 2, 2)), dma((halves, 2, 2)),
             dma((halves,)), dma((halves,)), dma((halves,)), dma((2, 4)), dma((4,)),
+            pltpu.SemaphoreType.REGULAR((3, 2)),
         ],
         compiler_params=pltpu.CompilerParams(collective_id=0, has_side_effects=True),
     )(temporal_links, spatial_links, rotations)
-    transfer, log_scale = pl.pallas_call(
-        finish,
-        name="hand_over",
-        out_shape=(
-            jax.ShapeDtypeStruct((162, 2, 3 * LANES), f32),
-            jax.ShapeDtypeStruct((2, 3 * LANES), f32),
-        ),
-        in_specs=[pl.BlockSpec(memory_space=pl.ANY)] * 2,
-        out_specs=[pl.BlockSpec(memory_space=pl.ANY)] * 2,
-        scratch_shapes=[
-            pltpu.VMEM((162, 2, 3 * LANES), f32), pltpu.VMEM((2, 3 * LANES), f32),
-            dma((7,)), dma((7,)),
-        ],
-    )(transfer, log_scale)
     return transfer.reshape(2, 9, 9, 1, 2, 3 * LANES), log_scale.reshape(1, 2, 3 * LANES)
 
 

time: 67.7 us -> 65.5 us (0.968)
  Pallas kernels: 66.9 us -> 63.3 us
  local copies, waits for them, and re-layouts: 0 us -> 1.36 us
    pallas_call x2 -> x1, Pallas kernels: 66.9 us -> 63.3 us  [per_device(): pl.pallas_call(kernel, name='slab_chain', out_shape=(pltpu.VMEM((162, 2,...]
    unnamed x0 -> x2, local copies, waits for them, and re-layouts: none -> 1.36 us
where the time goes in v3:
time: 65.5 us; the launch traced here: 65.3 us
  Pallas kernels  63.3 us (97%)
  local copies, waits for them, and re-layouts  1.36 us (2%)
    pallas_call x1, Pallas kernels, per_device(): pl.pallas_call(kernel, name='slab_chain', out_shape=(pltpu.VMEM((162, 2,...  63.3 us
    unnamed x2, local copies, waits for them, and re-layouts  1.36 us

profile of v3, /device:TPU:6, one launch (start us, length us, event | category | flops | bytes accessed | tf_op | source)
XLA Modules:
  0.0 65.3 jit_solution(18171848290904358448)
XLA Ops:
  0.6 63.3 %slab_chain.1 = (f32[162,2,384]{2,1,0:T(2,128)S(1)}, f32[2,384]{1,0:T(2,128)S(1)}) custom-call(f32[18,4,2,384]{3,2,1,0:T(2,128)} %time_hbm.1, f32[3,18,4,2,384]{4,3,2,1,0:T(2,128)} %space_hbm.1, f32[3,3,4,4,2,384]{5,4,3,2,1,0:T(2,128)} %turn_hbm.1), custom_call_target="tpu_custom_call" | custom-call | tf_op jit(solution)/shard_map/slab_chain/pallas_call | solution.py:609
  64.0 0.8 %copy.8 = f32[2,9,9,1,2,384]{5,4,3,2,1,0:T(2,128)} copy(f32[2,9,9,1,2,384]{5,4,3,2,1,0:T(2,128)S(1)} %bitcast.4) | data formatting | bytes 995328
  64.7 0.6 copy.9

commit v4 on v3

--- a/solution.py
+++ b/solution.py
@@ -172,6 +172,9 @@
             lanes, rows = pl.ds(LANES * j, LANES), pl.ds(8 * t + 2 * j, 2)
             pltpu.make_async_copy(
                 time_hbm.at[:, t, :, lanes], time_raw.at[:, rows, :], in_sem.at[0]).start()
+    for t in range(4):
+        for j in range(3):
+            lanes, rows = pl.ds(LANES * j, LANES), pl.ds(8 * t + 2 * j, 2)
             pltpu.make_async_copy(
                 space_hbm.at[:, :, t, :, lanes], space_raw.at[:, :, rows, :], in_sem.at[1]).start()
     for t in range(4):
@@ -235,11 +238,6 @@
         landed(pack_in.at[number, block, side, :, pl.ds(0, 6), :], sem.at[number, block, side])
 
     two_rows = [*range(6), *range(9, 15)]
-    landed(space_raw.at[:, :, pl.ds(0, 24), :], in_sem.at[1])
-    for block in range(2):
-        for place, entry in enumerate(two_rows):
-            left_out[place, pl.ds(8 * block, 8), :] = (
-                space_raw[0, entry, pl.ds(16 * block + 1, 8, stride=2), :])
     landed(time_raw.at[:, pl.ds(0, 24), :], in_sem.at[0])
     for block in range(2):
         packed = []
@@ -255,6 +253,11 @@
     for block in range(2):
         for side, target in ((0, left), (1, right)):
             send_halo(0, block, side, target)
+    landed(space_raw.at[:, :, pl.ds(0, 24), :], in_sem.at[1])
+    for block in range(2):
+        for place, entry in enumerate(two_rows):
+            left_out[place, pl.ds(8 * block, 8), :] = (
+                space_raw[0, entry, pl.ds(16 * block + 1, 8, stride=2), :])
     edges = []
     for t in range(4):
         rows = pl.ds(4 * t, 3)
@@ -453,10 +456,11 @@
             send_loops(sweep, parity)
 
     def normalized(load, store, log):
-        square = None
-        for k in range(162):
+        squares = [load(k) * load(k) for k in range(6)]
+        for k in range(6, 162):
             value = load(k)
-            square = value * value if square is None else square + value * value
+            squares[k % 6] = squares[k % 6] + value * value
+        square = (squares[0] + squares[1]) + (squares[2] + squares[3]) + (squares[4] + squares[5])
         rms = jnp.sqrt(square / 162.0 + 1e-06)
         inv = 1.0 / rms
         for k in range(162):

time: 65.5 us -> 64.5 us (0.985)
  Pallas kernels: 63.3 us -> 62.3 us
    pallas_call x1, Pallas kernels: 63.3 us -> 62.3 us  [per_device(): pl.pallas_call(kernel, name='slab_chain', out_shape=(pltpu.VMEM((162, 2,...]
where the time goes in v4:
time: 64.5 us; the launch traced here: 64.3 us
  Pallas kernels  62.3 us (97%)
  local copies, waits for them, and re-layouts  1.36 us (2%)
    pallas_call x1, Pallas kernels, per_device(): pl.pallas_call(kernel, name='slab_chain', out_shape=(pltpu.VMEM((162, 2,...  62.3 us
    unnamed x2, local copies, waits for them, and re-layouts  1.36 us

profile of v4, /device:TPU:6, one launch (start us, length us, event | category | flops | bytes accessed | tf_op | source)
XLA Modules:
  0.0 64.3 jit_solution(7166658852730421931)
XLA Ops:
  0.6 62.3 %slab_chain.1 = (f32[162,2,384]{2,1,0:T(2,128)S(1)}, f32[2,384]{1,0:T(2,128)S(1)}) custom-call(f32[18,4,2,384]{3,2,1,0:T(2,128)} %time_hbm.1, f32[3,18,4,2,384]{4,3,2,1,0:T(2,128)} %space_hbm.1, f32[3,3,4,4,2,384]{5,4,3,2,1,0:T(2,128)} %turn_hbm.1), custom_call_target="tpu_custom_call" | custom-call | tf_op jit(solution)/shard_map/slab_chain/pallas_call | solution.py:613
  63.0 0.8 %copy.8 = f32[2,9,9,1,2,384]{5,4,3,2,1,0:T(2,128)} copy(f32[2,9,9,1,2,384]{5,4,3,2,1,0:T(2,128)S(1)} %bitcast.4) | data formatting | bytes 995328
  63.8 0.6 copy.9

commit v5 on v4

--- a/solution.py
+++ b/solution.py
@@ -496,10 +496,10 @@
 
     def result_to(target):
         lanes = pl.ds(pl.multiple_of(LANES * (ix - 1), LANES), LANES)
-        rows = pl.ds(2 * target, 2)
+        rows, stage = pl.ds(2 * target, 2), min(target, 2)
         return (
-            (final.at[pl.ds(0, 162), rows, :], out_hbm.at[:, :, lanes]),
-            (final.at[162, rows, :], log_hbm.at[:, lanes]))
+            (final.at[stage, pl.ds(0, 162), rows, :], out_hbm.at[:, :, lanes]),
+            (final.at[stage, 162, rows, :], log_hbm.at[:, lanes]))
 
     @pl.when(ix > 0)
     def _():
@@ -557,16 +557,7 @@
             swapped = jnp.where(row % 2 == 0, turn_rows(value, 1), turn_rows(value, -1))
             return jnp.where(odd, swapped, value)
 
-        for k in range(163):
-            chain_a[k] = moved(oper[nz - 1, k], k, 2)
-            chain_b[k] = moved(chain_a[k], k, 2)
-        combine(chain_b, chain_a, group, lambda k, value: jnp.where(row < 2, chain_a[k], value))
-        for k in range(163):
-            chain_b[k] = moved(group[k], k, 4)
-        combine(chain_b, group, chain_a, lambda k, value: jnp.where(row < 4, group[k], value))
-        combine(chain_a, oper.at[iz], final, by_column)
-
-        for target in range(nx):
+        def send_result(target):
             @pl.when(ix == target)
             def _():
                 for piece, (src, dst) in enumerate(result_to(target)):
@@ -578,14 +569,36 @@
                     remote(
                         src, dst, done_sem.at[2 + piece], back_sem.at[piece, ix], (target, iz, ia)
                     ).start()
+
+        for k in range(163):
+            chain_a[k] = moved(oper[nz - 1, k], k, 2)
+        combine(chain_a, oper.at[iz], group, lambda k, value: value)
+        for k in range(163):
+            final[0, k] = by_column(k, group[k])
+        send_result(0)
+        for k in range(163):
+            chain_b[k] = moved(chain_a[k], k, 2)
+        combine(chain_b, group, chain_a, lambda k, value: value)
+        for k in range(163):
+            final[1, k] = by_column(k, chain_a[k])
+        send_result(1)
+        for k in range(163):
+            group[k] = moved(chain_b[k], k, 2)
+        log = normalized(
+            lambda k: group[k],
+            lambda k, value: group.__setitem__(k, jnp.where(row < 6, group[k], value)), group[162])
+        group[162] = jnp.where(row < 6, group[162], log)
+        combine(group, chain_a, final.at[2], by_column)
+        send_result(2)
+        send_result(3)
         for piece, (src, dst) in enumerate(result_to(0)):
             pltpu.make_async_copy(src, dst, done_sem.at[piece]).wait()
 
     for source in range(1, nx):
         @pl.when(ix != source)
         def _():
-            landed(final.at[pl.ds(0, 162), pl.ds(0, 2), :], back_sem.at[0, source])
-            landed(final.at[162, pl.ds(0, 2), :], back_sem.at[1, source])
+            landed(final.at[0, pl.ds(0, 162), pl.ds(0, 2), :], back_sem.at[0, source])
+            landed(final.at[0, 162, pl.ds(0, 2), :], back_sem.at[1, source])
 
     for piece, cover in enumerate(covers):
         landed(cover, edge_out.at[piece])
@@ -603,8 +616,8 @@
     def _():
         for number in range(halves):
             landed(space_raw.at[0, :, pl.ds(0, 11), :], loop_sent.at[number])
-        landed(final.at[pl.ds(0, 162), pl.ds(0, 6), :], done_sem.at[2])
-        landed(final.at[162, pl.ds(0, 6), :], done_sem.at[3])
+        landed(final.at[0, pl.ds(0, 162), pl.ds(0, 6), :], done_sem.at[2])
+        landed(final.at[0, 162, pl.ds(0, 6), :], done_sem.at[3])
 
 
 def per_device(temporal_links, spatial_links, rotations):
@@ -636,7 +649,7 @@
             pltpu.VMEM((163, 8, LANES), f32),
             pltpu.VMEM((163, 8, LANES), f32),
             pltpu.VMEM((81, 8, LANES), f32),
-            pltpu.VMEM((163, 8, LANES), f32),
+            pltpu.VMEM((3, 163, 8, LANES), f32),
             dma((3,)), dma((4,)), dma((4,)), dma((halves, 2, 2)), dma((halves, 2, 2)),
             dma((halves,)), dma((halves,)), dma((halves,)), dma((2, 4)), dma((4,)),
             pltpu.SemaphoreType.REGULAR((3, 2)),

time: 64.5 us -> 63.3 us (0.981)
  Pallas kernels: 62.3 us -> 60.9 us
    pallas_call x1, Pallas kernels: 62.3 us -> 60.9 us  [per_device(): pl.pallas_call(kernel, name='slab_chain', out_shape=(pltpu.VMEM((162, 2,...]
where the time goes in v5:
time: 63.3 us; the launch traced here: 62.9 us
  Pallas kernels  60.9 us (96%)
  local copies, waits for them, and re-layouts  1.36 us (2%)
  between operations  0.64 us (1%)
    pallas_call x1, Pallas kernels, per_device(): pl.pallas_call(kernel, name='slab_chain', out_shape=(pltpu.VMEM((162, 2,...  60.9 us
    unnamed x2, local copies, waits for them, and re-layouts  1.36 us

profile of v5, /device:TPU:6, one launch (start us, length us, event | category | flops | bytes accessed | tf_op | source)
XLA Modules:
  0.0 62.9 jit_solution(13293059313854670786)
XLA Ops:
  0.6 60.9 %slab_chain.1 = (f32[162,2,384]{2,1,0:T(2,128)S(1)}, f32[2,384]{1,0:T(2,128)S(1)}) custom-call(f32[18,4,2,384]{3,2,1,0:T(2,128)} %time_hbm.1, f32[3,18,4,2,384]{4,3,2,1,0:T(2,128)} %space_hbm.1, f32[3,3,4,4,2,384]{5,4,3,2,1,0:T(2,128)} %turn_hbm.1), custom_call_target="tpu_custom_call" | custom-call | tf_op jit(solution)/shard_map/slab_chain/pallas_call | solution.py:626
  61.6 0.8 %copy.8 = f32[2,9,9,1,2,384]{5,4,3,2,1,0:T(2,128)} copy(f32[2,9,9,1,2,384]{5,4,3,2,1,0:T(2,128)S(1)} %bitcast.4) | data formatting | bytes 995328
  62.4 0.6 copy.9
